TPU v7x, 32 devices: a whole 2x2x4 slice. The times are simulated.
32 devices in a mesh: dp: 8 (over z, y), comp: 4 (over x, core).
Axes of the slice: x: 2, y: 2, z: 4, core: 2. Of those that a mesh axis runs over, the one named last changes fastest.
Arguments:
- points: float32 [8192, 64], P('dp'), may hold values from -36 to 36
- means: float32 [256, 64], P('comp'), may hold values from -6 to 6
- whiten: float32 [256, 64, 64], P('comp'), may hold values from -0.25 to 2, as said below
- log_weight: float32 [256], P('comp'), may hold values from -4 to 4
Outputs:
- new_means: float32 [256, 64], P('comp')
- new_whiten: float32 [256, 64, 64], P('comp')
- new_log_weight: float32 [256], P('comp')
- point_loglik: float32 [8192], P('dp')
Inputs may be any that keep to these rules, and one draw needn't show every extreme that they name: Each whiten[k] is lower triangular with diagonal entries between 0.5 and 2.
All inputs are finite; a program needn't handle non-finite values.
Results may differ from a plain program's by a relative error of at most 0.0003.
Values sent between devices are 32-bit elements; how exact they have to be, the bound alone decides.
A program may use at most 64 MiB of HBM per device.

v0:
```python
import math
import jax
import jax.numpy as jnp
from jax import lax
from jax.sharding import PartitionSpec as P

K = 256
HIGH = lax.Precision.HIGHEST


def refit_params(square, sums, counts, width, total_points):
    grown = counts + 1.0
    centre = sums / grown[:, None]
    eye = jnp.eye(width, dtype=jnp.float32)
    cov = (square - sums[:, :, None] * sums[:, None, :] / grown[:, None, None] + eye[None]) / grown[
        :, None, None
    ]
    chol = jnp.linalg.cholesky(cov)
    factor = lax.linalg.triangular_solve(
        chol, jnp.broadcast_to(eye, chol.shape), left_side=True, lower=True
    )
    weight = jnp.log(grown / (total_points + K))
    return (centre, factor, weight)


def body(points, means, whiten, log_weight):
    count_rows, width = points.shape
    local = means.shape[0]
    block = min(512, count_rows)
    blocks = count_rows // block
    stacked = whiten.reshape(local * width, width)
    offset = jnp.einsum("ked,kd->ke", whiten, means, precision=HIGH).reshape(local * width, 1)
    logdet = jnp.sum(jnp.log(jnp.diagonal(whiten, axis1=1, axis2=2)), axis=1)
    const = log_weight + logdet - 0.5 * width * math.log(2.0 * math.pi)
    tiles = points.reshape(blocks, block, width)

    def score(tile):
        projected = (
            lax.dot_general(stacked, tile, (((1,), (1,)), ((), ())), precision=HIGH) - offset
        )
        distance = jnp.sum((projected * projected).reshape(local, width, block), axis=1)
        return const[:, None] - 0.5 * distance

    logp = lax.map(score, tiles)
    peak = jnp.max(logp, axis=1)
    peak = lax.pmax(peak, "comp")
    partial_total = jnp.sum(jnp.exp(logp - peak[:, None, :]), axis=1)
    total = lax.psum(partial_total, "comp")
    lse = peak + jnp.log(total)
    resp = jnp.exp(logp - lse[:, None, :])

    def accumulate(carry, pieces):
        tile, weight = pieces
        outer = (tile[:, :, None] * tile[:, None, :]).reshape(block, width * width)
        scatter = carry[0] + jnp.dot(weight, outer, precision=HIGH)
        sums = carry[1] + jnp.dot(weight, tile, precision=HIGH)
        counts = carry[2] + jnp.sum(weight, axis=1)
        return ((scatter, sums, counts), None)

    columns = width * width
    start = (
        jnp.zeros((local, columns), jnp.float32),
        jnp.zeros((local, width), jnp.float32),
        jnp.zeros((local,), jnp.float32),
    )
    (scatter, sums, counts), unused = lax.scan(accumulate, start, (tiles, resp))
    total_points = count_rows * lax.axis_size("dp")
    scatter, sums, counts = (
        lax.psum_scatter(scatter, "dp", scatter_dimension=0, tiled=True),
        lax.psum_scatter(sums, "dp", scatter_dimension=0, tiled=True),
        lax.psum_scatter(counts, "dp", scatter_dimension=0, tiled=True),
    )
    centre, factor, weight = refit_params(
        scatter.reshape(scatter.shape[0], width, width), sums, counts, width, total_points
    )
    centre, factor, weight = (
        lax.all_gather(centre, "dp", axis=0, tiled=True),
        lax.all_gather(factor, "dp", axis=0, tiled=True),
        lax.all_gather(weight, "dp", axis=0, tiled=True),
    )
    return (centre, factor, weight, (lse / width).reshape(count_rows))


def solution(mesh):
    in_specs = (P("dp", None), P("comp", None), P("comp", None, None), P("comp"))
    out_specs = (P("comp", None), P("comp", None, None), P("comp"), P("dp"))
    return jax.shard_map(body, mesh=mesh, in_specs=in_specs, out_specs=out_specs, check_vma=False)
```

profile of v0, /device:TPU:0, one launch (start us, length us, event | category | flops | bytes accessed | tf_op | source)
XLA Modules:
  0.0 330.3 jit_solution(15399564940060556085)
XLA Ops:
  7.3 1.2 reshape.97
  8.4 2.4 copy.41
  10.8 0.9 gather_fusion
  11.7 4.9 %fusion.15 = f32[64,1,64]{2,1,0:T(1,128)S(1)} fusion(f32[64,64,64]{2,1,0:T(8,128)} %param.10, f32[64,64,1]{1,2,0:T(1,128)S(1)} %bitcast.74), kind=kOutput, calls=%fused_computation.45 | convolution fusion | flops 3145728 | bytes 1081344 | tf_op jit(solution)/shard_map/ked,kd->ke/dot_general | solution.py:32
  16.8 0.7 add_add_fusion
  17.4 50.3 %while.25 = (s32[]{:T(128)}, f32[2,64,512]{2,1,0:T(8,128)}, f32[64]{0:T(128)S(1)}, f32[2,512,64]{1,0,2:T(2,128)S(1)}, f32[4096,64]{1,0:T(8,128)}, /*index=5*/f32[4096,1]{0,1:T(1,128)S(1)}, s32[]{:T(128)}) while((s32[]{:T(128)}, f32[2,64,512]{2,1,0:T(8,128)}, f32[64]{0:T(128)S(1)}, f32[2,512,64]{1,0,2:T(2,128)S(1)}, f32[4096,64]{1,0:T(8,128)}, ...), condition=%wide.region_3.4_spmd, body=%wide.region_1.3_spmd.sunk | while | flops 1616936960 | bytes 37765772 | solution.py:44
  17.6 0.1 copy.63
  17.7 10.3 %multiply_bitcast_fusion.3 = f32[4096,512]{0,1:T(8,128)} fusion(f32[4096,64]{1,0:T(8,128)} %get-tuple-element.263, f32[4096]{0:T(1024)S(1)} %bitcast.78, f32[1,512,64]{2,1,0:T(8,128)S(1)} %copy.63), kind=kOutput, calls=%fused_computation.2.clone.1 | convolution fusion | flops 1614807040 | bytes 9584640 | tf_op jit(solution)/shard_map/while/body/eval_jaxpr/dot_general | solution.py:39
  28.0 9.0 %copy.64 = f32[4096,512]{1,0:T(8,128)} copy(f32[4096,512]{0,1:T(8,128)} %multiply_bitcast_fusion.3) | data formatting | bytes 16777216 | tf_op jit(solution)/shard_map/while/body/eval_jaxpr/mul | solution.py:41
  37.0 4.8 %bitcast_reduce_fusion.2 = f32[64,512]{1,0:T(8,128)S(1)} fusion(f32[4096,512]{1,0:T(8,128)} %copy.64), kind=kLoop, calls=%fused_computation.1.clone.1 | loop fusion | flops 2064384 | bytes 8519680 | tf_op jit(solution)/shard_map/while/body/eval_jaxpr/reduce_sum | solution.py:41
  41.9 0.7 copy-done.3
  42.7 0.1 copy.63
  42.8 10.3 %multiply_bitcast_fusion.3 = f32[4096,512]{0,1:T(8,128)} fusion(f32[4096,64]{1,0:T(8,128)} %get-tuple-element.263, f32[4096]{0:T(1024)S(1)} %bitcast.78, f32[1,512,64]{2,1,0:T(8,128)S(1)} %copy.63), kind=kOutput, calls=%fused_computation.2.clone.1 | convolution fusion | flops 1614807040 | bytes 9584640 | tf_op jit(solution)/shard_map/while/body/eval_jaxpr/dot_general | solution.py:39
  53.2 9.0 %copy.64 = f32[4096,512]{1,0:T(8,128)} copy(f32[4096,512]{0,1:T(8,128)} %multiply_bitcast_fusion.3) | data formatting | bytes 16777216 | tf_op jit(solution)/shard_map/while/body/eval_jaxpr/mul | solution.py:41
  62.1 4.8 %bitcast_reduce_fusion.2 = f32[64,512]{1,0:T(8,128)S(1)} fusion(f32[4096,512]{1,0:T(8,128)} %copy.64), kind=kLoop, calls=%fused_computation.1.clone.1 | loop fusion | flops 2064384 | bytes 8519680 | tf_op jit(solution)/shard_map/while/body/eval_jaxpr/reduce_sum | solution.py:41
  67.0 0.7 copy-done.3
  67.7 1.0 reduce_max.9
  68.7 8.4 %pmax.7 = f32[2,512]{1,0:T(2,128)S(1)} all-reduce(f32[2,512]{1,0:T(2,128)S(1)} %reduce_max.9), channel_id=1, replica_groups=mesh['dp'=8,'comp'=4] {'comp'}, use_global_device_ids=true, to_apply=%region_5.6 | all-reduce | flops 1024 | bytes 8192 | tf_op jit(solution)/shard_map/pmax | solution.py:46
  77.1 1.0 exponential_reduce_fusion
  78.1 5.8 %psum.7 = f32[2,512]{1,0:T(2,128)S(1)} all-reduce(f32[2,512]{1,0:T(2,128)S(1)} %exponential_reduce_fusion), channel_id=1, replica_groups=mesh['dp'=8,'comp'=4] {'comp'}, use_global_device_ids=true, to_apply=%region_7.8 | all-reduce | flops 1024 | bytes 8192 | tf_op jit(solution)/shard_map/psum | solution.py:48
  83.9 1.0 subtract_exponential_fusion
  84.9 30.5 %while.26 = (s32[]{:T(128)}, f32[64,4096]{1,0:T(8,128)S(1)}, f32[64,64]{1,0:T(8,128)S(1)}, f32[64]{0:T(128)S(1)}, f32[2,64,512]{2,1,0:T(8,128)S(1)}, /*index=5*/f32[2,512,64]{1,0,2:T(2,128)S(1)}, s32[]{:T(128)}, s32[]{:T(128)}) while((s32[]{:T(128)}, f32[64,4096]{1,0:T(8,128)S(1)}, f32[64,64]{1,0:T(8,128)S(1)}, ...), condition=%wide.region_10.11_spmd.clone, body=%wide.region_8.10_spmd.clone.sunk | while | flops 1638441088 | bytes 20104304 | solution.py:66
  85.0 4.3 %broadcast_multiply_fusion.2 = f32[512,64,64]{0,2,1:T(8,128)} fusion(f32[512,64]{0,1:T(8,128)S(1)} %bitcast.77), kind=kLoop, calls=%fused_computation.8.clone.1 | loop fusion | flops 2097152 | bytes 8519680 | tf_op jit(solution)/shard_map/while/body/eval_jaxpr/mul | solution.py:54
  89.4 10.3 %convolution_add_fusion.4 = f32[64,4096]{1,0:T(8,128)S(1)} fusion(f32[512,4096]{0,1:T(8,128)} %bitcast.75, f32[64,4096]{1,0:T(8,128)S(1)} %get-tuple-element.275, pred[]{:T(512)S(6)} %compare.11, f32[2,64,512]{2,1,0:T(8,128)S(1)} %get-tuple-element.286, s32[]{:T(128)} %get-tuple-element.274), kind=kOutput, calls=%fused_computation.7.clone.1 | convolution fusion | flops 1611137024 | bytes 10616837 | tf_op jit(solution)/shard_map/while/body/eval_jaxpr/dot_general | solution.py:55
  99.7 0.3 convolution_add_fusion.5
  100.3 4.3 %broadcast_multiply_fusion.2 = f32[512,64,64]{0,2,1:T(8,128)} fusion(f32[512,64]{0,1:T(8,128)S(1)} %bitcast.77), kind=kLoop, calls=%fused_computation.8.clone.1 | loop fusion | flops 2097152 | bytes 8519680 | tf_op jit(solution)/shard_map/while/body/eval_jaxpr/mul | solution.py:54
  104.6 10.3 %convolution_add_fusion.4 = f32[64,4096]{1,0:T(8,128)S(1)} fusion(f32[512,4096]{0,1:T(8,128)} %bitcast.75, f32[64,4096]{1,0:T(8,128)S(1)} %get-tuple-element.275, pred[]{:T(512)S(6)} %compare.11, f32[2,64,512]{2,1,0:T(8,128)S(1)} %get-tuple-element.286, s32[]{:T(128)} %get-tuple-element.274), kind=kOutput, calls=%fused_computation.7.clone.1 | convolution fusion | flops 1611137024 | bytes 10616837 | tf_op jit(solution)/shard_map/while/body/eval_jaxpr/dot_general | solution.py:55
  114.9 0.3 convolution_add_fusion.5
  115.4 1.0 copy-done.1
  116.5 0.6 fusion.14
  118.4 21.9 %all-reduce.2 = f32[64]{0:T(128)S(1)} all-reduce(f32[64]{0:T(128)S(1)} %get-tuple-element.72), channel_id=3, replica_groups=mesh['dp'=8,'comp'=4] {'dp'}, use_global_device_ids=true, to_apply=%region_12.13.clone | all-reduce | flops 64 | bytes 512
  140.3 0.2 log_dynamic-update-slice_fusion
  140.5 33.9 %all-reduce.3 = (f32[64,64]{1,0:T(8,128)S(1)}, f32[64]{0:T(128)}) all-reduce(f32[64,64]{1,0:T(8,128)S(1)} %get-tuple-element.71, f32[64]{0:T(128)S(1)} %get-tuple-element.167), channel_id=2, replica_groups=mesh['dp'=8,'comp'=4] {'dp'}, use_global_device_ids=true, to_apply=%region_11.12.clone | all-reduce | flops 4160 | bytes 33280
  174.5 7.4 %reduce-scatter.2.cloned.1.call-done = f32[8,4096]{1,0:T(8,128)} async-done(((f32[64,4096]{1,0:T(8,128)}), f32[8,4096]{1,0:T(8,128)}) %reduce-scatter.2.cloned.1.call-update) | async-done | bytes 131088 | tf_op jit(solution)/shard_map/reduce_scatter | solution.py:69
  181.9 1.0 reshape.100
  182.9 0.1 copy.44
  183.0 0.1 add_divide_fusion
  183.2 0.1 copy.46
  183.3 0.1 fusion.11
  183.5 46.9 %custom-call.7 = f32[8,64,64]{2,1,0:T(8,128)S(1)} custom-call(f32[8,64,64]{2,1,0:T(8,128)S(1)} %fusion.11), custom_call_target="Cholesky" | custom-call | tf_op jit(solution)/shard_map/jit(cholesky)/cholesky | solution.py:18
  230.4 0.1 compare_reduce_fusion
  230.7 39.3 %custom-call.8 = f32[8,1,64,64]{2,3,1,0:T(8,128)S(1)} custom-call(f32[8,1,64,64]{3,2,1,0:T(8,128)S(1)} %select_bitcast_fusion), custom_call_target="InvertDiagBlocksLowerTriangular" | custom-call | tf_op jit(solution)/shard_map/triangular_solve | solution.py:19
  270.0 1.3 fusion.9
  271.3 30.9 %all_gather.9 = f32[64,64]{1,0:T(8,128)S(1)} all-gather(f32[8,64]{1,0:T(8,128)S(1)} %get-tuple-element.165), channel_id=1, replica_groups=mesh['dp'=8,'comp'=4] {'dp'}, dimensions={0}, use_global_device_ids=true | all-gather | bytes 18432 | tf_op jit(solution)/shard_map/all_gather | solution.py:77
  302.2 0.6 copy.55
  302.8 16.9 %all-gather.2.cloned.1.call-done = f32[64,64,64]{2,1,0:T(8,128)} async-done(((f32[8,64,64]{2,1,0:T(8,128)}), f32[64,64,64]{2,1,0:T(8,128)}) %all-gather.2.cloned.1.call-update) | async-done | bytes 1048592 | tf_op jit(solution)/shard_map/all_gather | solution.py:78
  319.7 0.6 copy.89
  320.3 3.2 copy.90
  (43 shorter events, 1.5 us)
Async XLA Ops:
  7.2 4.6 %copy-start = (f32[64,64]{1,0:T(8,128)S(1)}, f32[64,64]{1,0:T(8,128)}, u32[]{:S(2)}) copy-start(f32[64,64]{1,0:T(8,128)} %param.9) | copy-start | bytes 49156
  7.2 174.7 %reduce-scatter.2.cloned.1.call-start = ((), (), s32[]{:S(2)}) async-start(), calls=%async_computation.1 | async-start | bytes 1179648 | tf_op jit(solution)/shard_map/reduce_scatter | solution.py:69
  37.0 4.8 %copy-start.2 = (f32[2,64,512]{2,1,0:T(8,128)S(1)}, f32[2,64,512]{2,1,0:T(8,128)}, u32[]{:S(2)}) copy-start(f32[2,64,512]{2,1,0:T(8,128)} %get-tuple-element.253) | copy-start | bytes 786436 | tf_op jit(solution)/shard_map/while
  41.9 0.7 copy-start.3
  62.1 4.8 %copy-start.2 = (f32[2,64,512]{2,1,0:T(8,128)S(1)}, f32[2,64,512]{2,1,0:T(8,128)}, u32[]{:S(2)}) copy-start(f32[2,64,512]{2,1,0:T(8,128)} %get-tuple-element.253) | copy-start | bytes 786436 | tf_op jit(solution)/shard_map/while
  67.0 0.7 copy-start.3
  84.9 31.7 %copy-start.4 = (u32[32]{0:T(128)S(1)}, u32[32]{0:T(128)}, u32[]{:S(2)}) copy-start(u32[32]{0:T(128)} %constant.106) | copy-start | bytes 388
  115.4 1.0 copy-start.1
  116.4 203.3 %all-gather.2.cloned.1.call-start = ((), (), s32[]{:S(2)}) async-start(), calls=%async_computation.2 | async-start | bytes 2359296 | tf_op jit(solution)/shard_map/all_gather | solution.py:78
Sparse Core Ops, SparseCore 0:
  116.5 65.3 reduce-scatter.1
  271.5 48.1 all-gather.1
where the time goes:
time: 331 us; the launch traced here: 330 us
  other arithmetic  109 us (33%)
  blocking collectives  101 us (31%)
  matrix products  48.1 us (15%)
  local copies, waits for them, and re-layouts  31.9 us (10%)
  waiting for transfers between devices  24.3 us (7%)
  between operations  15.5 us (5%)
    unnamed x2, blocking collectives  55.8 us
    another operation x4, other arithmetic, refit_params(): chol = jnp.linalg.cholesky(cov)  47.1 us
    another operation x3, other arithmetic, refit_params(): lax.linalg.triangular_solve(chol, jnp.broadcast_to(eye, chol.shape), left...  39.4 us
    all_gather x1, blocking collectives, body(): lax.all_gather(centre, 'dp', axis=0, tiled=True)  30.9 us
    dot_general x2, matrix products, accumulate(): scatter = carry[0] + jnp.dot(weight, outer, precision=HIGH)  20.7 us
    dot_general x2, matrix products, score(): lax.dot_general(stacked, tile, (((1,), (1,)), ((), ())), precision=HIGH)  20.6 us
    mul x2, local copies, waits for them, and re-layouts, score(): projected * projected  18 us
    all_gather x1, waiting for transfers between devices, body(): lax.all_gather(factor, 'dp', axis=0, tiled=True)  16.9 us
  transfers between devices with their start and end apart: 2, of which 2 were waited for; matrix products, arithmetic and copies ran while one was open for 0% of the time, Pallas kernels for 0%

commit v1 on v0

--- a/solution.py
+++ b/solution.py
@@ -6,6 +6,18 @@
 
 K = 256
 HIGH = lax.Precision.HIGHEST
+
+
+def gather_by_bits(x, axis, dim):
+    ways, here, step = (lax.axis_size(axis), lax.axis_index(axis), x.shape[dim])
+    line, have = (x, 1)
+    while have < ways:
+        line = jnp.concatenate(
+            [line, lax.ppermute(line, axis, [(d, (d - have) % ways) for d in range(ways)])],
+            axis=dim,
+        )
+        have = 2 * have
+    return jnp.roll(line, here * step, axis=dim)
 
 
 def refit_params(square, sums, counts, width, total_points):
@@ -75,7 +87,7 @@
     )
     centre, factor, weight = (
         lax.all_gather(centre, "dp", axis=0, tiled=True),
-        lax.all_gather(factor, "dp", axis=0, tiled=True),
+        gather_by_bits(factor, "dp", 0),
         lax.all_gather(weight, "dp", axis=0, tiled=True),
     )
     return (centre, factor, weight, (lse / width).reshape(count_rows))

time: 331 us -> 377 us (1.14)
  blocking collectives: 101 us -> 137 us
  local copies, waits for them, and re-layouts: 31.9 us -> 42.8 us
  starting transfers between devices: 0.08 us -> 6.93 us
  matrix products: 48.1 us -> 44.1 us
  waiting for transfers between devices: 24.3 us -> 20.3 us
    all_gather x1, blocking collectives: 30.9 us -> 66.6 us  [body(): lax.all_gather(centre, 'dp', axis=0, tiled=True)]
    all_gather x1 -> x0, waiting for transfers between devices: 16.9 us -> none  [body(): lax.all_gather(factor, 'dp', axis=0, tiled=True)]
    ppermute x0 -> x3, waiting for transfers between devices: none -> 13.1 us  [gather_by_bits(): lax.ppermute(line, axis, [(d, (d - have) % ways) for d in range(ways)])]
    ppermute x0 -> x3, starting transfers between devices: none -> 6.89 us  [gather_by_bits(): lax.ppermute(line, axis, [(d, (d - have) % ways) for d in range(ways)])]
    unnamed x11 -> x20, local copies, waits for them, and re-layouts: 8.31 us -> 11.1 us
  transfers between devices with their start and end apart: 2 -> 4, of which waited for: 2 -> 3; matrix products, arithmetic and copies ran while one was open for 0% -> 1% of each run, Pallas kernels for 0% -> 0%
where the time goes in v1:
time: 377 us
  blocking collectives  137 us (36%)
  other arithmetic  110 us (29%)
  matrix products  44.1 us (12%)
  local copies, waits for them, and re-layouts  42.8 us (11%)
  waiting for transfers between devices  20.3 us (5%)
  between operations  15.6 us (4%)
  starting transfers between devices  6.93 us (2%)
    all_gather x1, blocking collectives, body(): lax.all_gather(centre, 'dp', axis=0, tiled=True)  66.6 us
    unnamed x2, blocking collectives  56 us
    another operation x4, other arithmetic, refit_params(): chol = jnp.linalg.cholesky(cov)  47.1 us
    another operation x3, other arithmetic, refit_params(): lax.linalg.triangular_solve(chol, jnp.broadcast_to(eye, chol.shape), left...  39.4 us
    dot_general x2, matrix products, accumulate(): scatter = carry[0] + jnp.dot(weight, outer, precision=HIGH)  20.7 us
    dot_general x2, matrix products, score(): lax.dot_general(stacked, tile, (((1,), (1,)), ((), ())), precision=HIGH)  18.2 us
    mul x2, local copies, waits for them, and re-layouts, score(): projected * projected  18 us
    ppermute x3, waiting for transfers between devices, gather_by_bits(): lax.ppermute(line, axis, [(d, (d - have) % ways) for d in range(ways)])  13.1 us
  transfers between devices with their start and end apart: 4, of which 3 were waited for; matrix products, arithmetic and copies ran while one was open for 1% of the time, Pallas kernels for 0%

profile of v1, /device:TPU:0, one launch (start us, length us, event | category | flops | bytes accessed | tf_op | source)
XLA Modules:
  0.0 376.7 jit_solution(1718755375665119143)
XLA Ops:
  7.3 1.3 reshape.97
  8.6 3.3 copy.41
  11.9 1.6 gather_fusion
  13.6 3.3 fusion.15
  17.0 52.2 %while.25 = (s32[]{:T(128)}, f32[2,64,512]{2,1,0:T(8,128)}, f32[64]{0:T(128)S(1)}, f32[2,512,64]{1,0,2:T(2,128)S(1)}, f32[4096,64]{1,0:T(8,128)S(1)}, /*index=5*/f32[4096,1]{0,1:T(1,128)S(1)}, s32[]{:T(128)}) while((s32[]{:T(128)}, f32[2,64,512]{2,1,0:T(8,128)}, f32[64]{0:T(128)S(1)}, f32[2,512,64]{1,0,2:T(2,128)S(1)}, ...), condition=%wide.region_3.4_spmd, body=%wide.region_1.3_spmd.sunk | while | flops 1616936960 | bytes 37766024 | solution.py:56
  17.7 0.8 constant_dynamic-slice_fusion.7
  18.5 1.0 copy.63
  19.5 9.1 %multiply_bitcast_fusion.3 = f32[4096,512]{0,1:T(8,128)} fusion(f32[4096,64]{1,0:T(8,128)S(1)} %get-tuple-element.265, f32[4096]{0:T(1024)S(1)} %bitcast.80, f32[1,512,64]{2,1,0:T(8,128)S(1)} %copy.63), kind=kOutput, calls=%fused_computation.2.clone.1 | convolution fusion | flops 1614807040 | bytes 9584640 | tf_op jit(solution)/shard_map/while/body/eval_jaxpr/dot_general | solution.py:51
  28.6 9.0 %copy.64 = f32[4096,512]{1,0:T(8,128)} copy(f32[4096,512]{0,1:T(8,128)} %multiply_bitcast_fusion.3) | data formatting | bytes 16777216 | tf_op jit(solution)/shard_map/while/body/eval_jaxpr/mul | solution.py:53
  37.6 4.8 %bitcast_reduce_fusion.2 = f32[64,512]{1,0:T(8,128)S(1)} fusion(f32[4096,512]{1,0:T(8,128)} %copy.64), kind=kLoop, calls=%fused_computation.1.clone.1 | loop fusion | flops 2064384 | bytes 8519680 | tf_op jit(solution)/shard_map/while/body/eval_jaxpr/reduce_sum | solution.py:53
  42.4 0.7 fusion.29
  43.8 0.8 constant_dynamic-slice_fusion.7
  44.6 1.0 copy.63
  45.6 9.1 %multiply_bitcast_fusion.3 = f32[4096,512]{0,1:T(8,128)} fusion(f32[4096,64]{1,0:T(8,128)S(1)} %get-tuple-element.265, f32[4096]{0:T(1024)S(1)} %bitcast.80, f32[1,512,64]{2,1,0:T(8,128)S(1)} %copy.63), kind=kOutput, calls=%fused_computation.2.clone.1 | convolution fusion | flops 1614807040 | bytes 9584640 | tf_op jit(solution)/shard_map/while/body/eval_jaxpr/dot_general | solution.py:51
  54.7 9.0 %copy.64 = f32[4096,512]{1,0:T(8,128)} copy(f32[4096,512]{0,1:T(8,128)} %multiply_bitcast_fusion.3) | data formatting | bytes 16777216 | tf_op jit(solution)/shard_map/while/body/eval_jaxpr/mul | solution.py:53
  63.7 4.8 %bitcast_reduce_fusion.2 = f32[64,512]{1,0:T(8,128)S(1)} fusion(f32[4096,512]{1,0:T(8,128)} %copy.64), kind=kLoop, calls=%fused_computation.1.clone.1 | loop fusion | flops 2064384 | bytes 8519680 | tf_op jit(solution)/shard_map/while/body/eval_jaxpr/reduce_sum | solution.py:53
  68.4 0.7 fusion.29
  69.2 1.0 reduce_max.9
  70.2 8.4 %pmax.7 = f32[2,512]{1,0:T(2,128)S(1)} all-reduce(f32[2,512]{1,0:T(2,128)S(1)} %reduce_max.9), channel_id=1, replica_groups=mesh['dp'=8,'comp'=4] {'comp'}, use_global_device_ids=true, to_apply=%region_5.6 | all-reduce | flops 1024 | bytes 8192 | tf_op jit(solution)/shard_map/pmax | solution.py:58
  78.5 1.0 exponential_reduce_fusion
  79.5 5.8 %psum.7 = f32[2,512]{1,0:T(2,128)S(1)} all-reduce(f32[2,512]{1,0:T(2,128)S(1)} %exponential_reduce_fusion), channel_id=1, replica_groups=mesh['dp'=8,'comp'=4] {'comp'}, use_global_device_ids=true, to_apply=%region_7.8 | all-reduce | flops 1024 | bytes 8192 | tf_op jit(solution)/shard_map/psum | solution.py:60
  85.3 1.0 subtract_exponential_fusion
  86.3 30.5 %while.26 = (s32[]{:T(128)}, f32[64,4096]{1,0:T(8,128)S(1)}, f32[64,64]{1,0:T(8,128)S(1)}, f32[64]{0:T(128)S(1)}, f32[2,64,512]{2,1,0:T(8,128)S(1)}, /*index=5*/f32[2,512,64]{1,0,2:T(2,128)S(1)}, s32[]{:T(128)}, s32[]{:T(128)}) while((s32[]{:T(128)}, f32[64,4096]{1,0:T(8,128)S(1)}, f32[64,64]{1,0:T(8,128)S(1)}, ...), condition=%wide.region_10.11_spmd.clone, body=%wide.region_8.10_spmd.clone.sunk | while | flops 1638441088 | bytes 20104304 | solution.py:78
  86.5 4.3 %broadcast_multiply_fusion.2 = f32[512,64,64]{0,2,1:T(8,128)} fusion(f32[512,64]{0,1:T(8,128)S(1)} %bitcast.79), kind=kLoop, calls=%fused_computation.8.clone.1 | loop fusion | flops 2097152 | bytes 8519680 | tf_op jit(solution)/shard_map/while/body/eval_jaxpr/mul | solution.py:66
  90.8 10.3 %convolution_add_fusion.4 = f32[64,4096]{1,0:T(8,128)S(1)} fusion(f32[512,4096]{0,1:T(8,128)} %bitcast.77, f32[64,4096]{1,0:T(8,128)S(1)} %get-tuple-element.277, pred[]{:T(512)S(6)} %compare.12, f32[2,64,512]{2,1,0:T(8,128)S(1)} %get-tuple-element.288, s32[]{:T(128)} %get-tuple-element.276), kind=kOutput, calls=%fused_computation.7.clone.1 | convolution fusion | flops 1611137024 | bytes 10616837 | tf_op jit(solution)/shard_map/while/body/eval_jaxpr/dot_general | solution.py:67
  101.7 4.3 %broadcast_multiply_fusion.2 = f32[512,64,64]{0,2,1:T(8,128)} fusion(f32[512,64]{0,1:T(8,128)S(1)} %bitcast.79), kind=kLoop, calls=%fused_computation.8.clone.1 | loop fusion | flops 2097152 | bytes 8519680 | tf_op jit(solution)/shard_map/while/body/eval_jaxpr/mul | solution.py:66
  106.1 10.3 %convolution_add_fusion.4 = f32[64,4096]{1,0:T(8,128)S(1)} fusion(f32[512,4096]{0,1:T(8,128)} %bitcast.77, f32[64,4096]{1,0:T(8,128)S(1)} %get-tuple-element.277, pred[]{:T(512)S(6)} %compare.12, f32[2,64,512]{2,1,0:T(8,128)S(1)} %get-tuple-element.288, s32[]{:T(128)} %get-tuple-element.276), kind=kOutput, calls=%fused_computation.7.clone.1 | convolution fusion | flops 1611137024 | bytes 10616837 | tf_op jit(solution)/shard_map/while/body/eval_jaxpr/dot_general | solution.py:67
  116.9 1.0 copy-done.2
  119.8 22.0 %all-reduce.2 = f32[64]{0:T(128)S(1)} all-reduce(f32[64]{0:T(128)S(1)} %get-tuple-element.72), channel_id=3, replica_groups=mesh['dp'=8,'comp'=4] {'dp'}, use_global_device_ids=true, to_apply=%region_12.13.clone | all-reduce | flops 64 | bytes 512
  142.0 33.9 %all-reduce.3 = (f32[64,64]{1,0:T(8,128)S(1)}, f32[64]{0:T(128)}) all-reduce(f32[64,64]{1,0:T(8,128)S(1)} %get-tuple-element.71, f32[64]{0:T(128)S(1)} %get-tuple-element.167), channel_id=2, replica_groups=mesh['dp'=8,'comp'=4] {'dp'}, use_global_device_ids=true, to_apply=%region_11.12.clone | all-reduce | flops 4160 | bytes 33280
  176.1 7.2 %reduce-scatter.2.cloned.1.call-done = f32[8,4096]{1,0:T(8,128)} async-done(((f32[64,4096]{1,0:T(8,128)}), f32[8,4096]{1,0:T(8,128)}) %reduce-scatter.2.cloned.1.call-update) | async-done | bytes 131088 | tf_op jit(solution)/shard_map/reduce_scatter | solution.py:81
  183.3 1.0 reshape.100
  184.9 46.9 %custom-call.7 = f32[8,64,64]{2,1,0:T(8,128)S(1)} custom-call(f32[8,64,64]{2,1,0:T(8,128)S(1)} %fusion.11), custom_call_target="Cholesky" | custom-call | tf_op jit(solution)/shard_map/jit(cholesky)/cholesky | solution.py:30
  232.1 39.3 %custom-call.8 = f32[8,1,64,64]{2,3,1,0:T(8,128)S(1)} custom-call(f32[8,1,64,64]{3,2,1,0:T(8,128)S(1)} %select_bitcast_fusion), custom_call_target="InvertDiagBlocksLowerTriangular" | custom-call | tf_op jit(solution)/shard_map/triangular_solve | solution.py:31
  271.4 1.3 constant_dynamic-update-slice_fusion.7
  272.7 2.2 collective-permute-start
  274.9 4.2 %collective-permute-done = f32[8,64,64]{2,1,0:T(8,128)S(1)} collective-permute-done((f32[8,64,64]{2,1,0:T(8,128)S(1)}, f32[8,64,64]{2,1,0:T(8,128)S(1)}, u32[]{:S(2)}, u32[]{:S(2)}) %collective-permute-start) | collective-permute-done | bytes 131104 | tf_op jit(solution)/shard_map/ppermute | solution.py:16
  279.1 2.8 collective-permute-start.1
  281.9 8.9 %collective-permute-done.1 = f32[16,64,64]{2,1,0:T(8,128)S(1)} collective-permute-done((f32[16,64,64]{2,1,0:T(8,128)S(1)}, f32[16,64,64]{2,1,0:T(8,128)S(1)}, u32[]{:S(2)}, u32[]{:S(2)}) %collective-permute-start.1) | collective-permute-done | bytes 262176 | tf_op jit(solution)/shard_map/ppermute | solution.py:16
  291.0 1.9 collective-permute-start.2
  292.9 66.6 %all_gather.6 = f32[64,64]{1,0:T(8,128)S(1)} all-gather(f32[8,64]{1,0:T(8,128)S(1)} %get-tuple-element.165), channel_id=1, replica_groups=mesh['dp'=8,'comp'=4] {'dp'}, dimensions={0}, use_global_device_ids=true | all-gather | bytes 18432 | tf_op jit(solution)/shard_map/all_gather | solution.py:89
  360.7 0.8 constant_dynamic-update-slice_fusion.5
  361.6 1.1 constant_dynamic-update-slice_fusion.4
  362.7 0.7 constant_dynamic-update-slice_fusion.3
  363.4 0.7 constant_dynamic-update-slice_fusion.2
  364.1 0.8 constant_dynamic-update-slice_fusion.1
  365.0 1.1 constant_dynamic-update-slice_fusion
  366.0 3.2 constant_dynamic-slice_fusion.3
  (59 shorter events, 6.5 us)
Async XLA Ops:
  7.2 6.4 %copy-start = (f32[64,64]{1,0:T(8,128)S(1)}, f32[64,64]{1,0:T(8,128)}, u32[]{:S(2)}) copy-start(f32[64,64]{1,0:T(8,128)} %param.9) | copy-start | bytes 49156
  7.2 6.4 %copy-start.1 = (f32[64,64,64]{2,1,0:T(8,128)S(1)}, f32[64,64,64]{2,1,0:T(8,128)}, u32[]{:S(2)}) copy-start(f32[64,64,64]{2,1,0:T(8,128)} %param.10) | copy-start | bytes 3145732
  7.2 9.8 %copy-start.6 = (f32[64]{0:T(128)S(1)}, f32[64]{0:T(128)}, u32[]{:S(2)}) copy-start(f32[64]{0:T(128)} %param.11) | copy-start | bytes 772
  7.2 176.1 %reduce-scatter.2.cloned.1.call-start = ((), (), s32[]{:S(2)}) async-start(), calls=%async_computation.1 | async-start | bytes 1179648 | tf_op jit(solution)/shard_map/reduce_scatter | solution.py:81
  17.0 0.7 copy-start.3
  37.6 5.5 %copy-start.4 = (f32[2,512,64]{1,0,2:T(2,128)S(1)}, f32[2,512,64]{1,0,2:T(2,128)}, u32[]{:S(2)}) copy-start(f32[2,512,64]{1,0,2:T(2,128)} %copy-done.3) | copy-start | bytes 786436 | tf_op jit(solution)/shard_map/while
  43.1 0.7 copy-start.3
  63.7 5.5 %copy-start.4 = (f32[2,512,64]{1,0,2:T(2,128)S(1)}, f32[2,512,64]{1,0,2:T(2,128)}, u32[]{:S(2)}) copy-start(f32[2,512,64]{1,0,2:T(2,128)} %copy-done.3) | copy-start | bytes 786436 | tf_op jit(solution)/shard_map/while
  86.3 31.6 %copy-start.5 = (u32[32]{0:T(128)S(1)}, u32[32]{0:T(128)}, u32[]{:S(2)}) copy-start(u32[32]{0:T(128)} %constant.135) | copy-start | bytes 388
  116.8 1.0 copy-start.2
  272.7 6.4 %collective-permute-start = (f32[8,64,64]{2,1,0:T(8,128)S(1)}, f32[8,64,64]{2,1,0:T(8,128)S(1)}, u32[]{:S(2)}, u32[]{:S(2)}) collective-permute-start(f32[8,64,64]{2,1,0:T(8,128)S(1)} %get-tuple-element.172), channel_id=1, source_target_pairs={{0,28},{4,0},{8,4},{12,8},{16,12},{20,16},{24,20},{28,24},{1,29},{... | collective-permute-start | bytes 393224 | tf_op jit(solution)/shard_map/ppermute | solution.py:16
  279.1 11.7 %collective-permute-start.1 = (f32[16,64,64]{2,1,0:T(8,128)S(1)}, f32[16,64,64]{2,1,0:T(8,128)S(1)}, u32[]{:S(2)}, u32[]{:S(2)}) collective-permute-start(f32[16,64,64]{2,1,0:T(8,128)S(1)} %pad_maximum_fusion.1), channel_id=1, source_target_pairs={{0,24},{4,28},{8,0},{12,4},{16,8},{20,12},{24,16},{28,20},{1,25},{... | collective-permute-start | bytes 786440 | tf_op jit(solution)/shard_map/ppermute | solution.py:16
  291.0 70.6 %collective-permute-start.2 = (f32[32,64,64]{2,1,0:T(8,128)S(1)}, f32[32,64,64]{2,1,0:T(8,128)S(1)}, u32[]{:S(2)}, u32[]{:S(2)}) collective-permute-start(f32[32,64,64]{2,1,0:T(8,128)S(1)} %pad_maximum_fusion), channel_id=1, source_target_pairs={{0,16},{4,20},{8,24},{12,28},{16,0},{20,4},{24,8},{28,12},{1,17},{... | collective-permute-start | bytes 1572872 | tf_op jit(solution)/shard_map/ppermute | solution.py:16
Sparse Core Ops, SparseCore 0:
  118.0 65.2 reduce-scatter.1
